TPU v7x, 256 devices: a 4x2x16 block of a 4x16x16 slice. The times are simulated.
256 devices in a mesh: groups: 2 (over y), seq: 16 (over z), tensor: 4 (over x), cfg: 2 (over core).
Axes of the slice: x: 4, y: 2, z: 16, core: 2. Of those that a mesh axis runs over, the one named last changes fastest.
The devices are a block of a 4x16x16 slice.
Arguments:
- latent: bfloat16 [8192, 3072], P(('groups', 'seq')), parts along dimension 0, may hold values from -6 to 6
- positions: int32 [3, 8192], P(None, ('groups', 'seq')), parts along dimension 1, may hold values from 0 to 79, as said below
- text_kv: bfloat16 [2, 2, 512, 3072], P('cfg', None, ('groups', 'seq'), 'tensor'), parts along dimension 2, may hold values from -6 to 6
- text_len: int32 [4], P(('groups', 'cfg')), parts along dimension 0, may hold values from 1 to 256
- modulation: float32 [3, 4, 3072], P(None, 'groups'), parts along dimension 1, may hold values from -3 to 3
- w_qkv: bfloat16 [3, 3072, 3072], P(None, 'cfg', 'tensor'), may hold values from -0.109375 to 0.109375
- norm_gains: float32 [2, 128], replicated, may hold values from 0.5 to 2.5
- w_out: bfloat16 [3072, 3072], P('tensor', 'cfg'), may hold values from -0.109375 to 0.109375
- guidance: float32 [2], P('groups'), parts along dimension 0, may hold values from 3 to 8
Outputs:
- guided: bfloat16 [8192, 3072], P(('groups', 'seq', 'tensor'), 'cfg'), parts along dimension 0
There are 2 independent parts, one for each index of `groups`. A program takes and returns all parts, laid end to end along the dimension named above; an argument that names none is the same for every part. Nothing has to cross between parts.
Inputs may be any that keep to these rules, and one draw needn't show every extreme that they name: `positions`: frame indices are below 33, height indices below 45, width indices below 80. `text_len`: text rows at or beyond the count are ignored.
All inputs are finite; a program needn't handle non-finite values.
Results may differ from a plain program's by a relative error of at most 0.018.
Values may be sent and summed in bfloat16 or wider, within the bound.
A program may use at most 128 MiB of HBM per device.

v0:
```python
import jax
import jax.numpy as jnp
from jax import lax
from jax.sharding import PartitionSpec as P

HEAD_DIM = 128


def in_blocks(shard, dim, devices):
    before, after = (shard.shape[:dim], shard.shape[dim + 1 :])
    return jnp.moveaxis(shard.reshape(*before, devices, -1, *after), dim, 0)


def summed_on_arrival(shard, axis, dim):
    devices = lax.axis_size(axis)
    tiles = lax.all_to_all(in_blocks(shard, dim, devices), axis, 0, 0, tiled=True)
    return jnp.sum(tiles.astype(jnp.float32), axis=0)


def side_by_side(arrays, axis, dim, along):
    ends, at = ([], 0)
    for a in arrays[:-1]:
        at += a.shape[along]
        ends.append(at)
    both = jnp.concatenate(arrays, axis=along)
    return tuple(jnp.split(lax.all_gather(both, axis, axis=dim, tiled=True), ends, axis=along))


def swapped(value, axis, apart):
    mask = 2**apart
    pairs = [(source, source ^ mask) for source in range(lax.axis_size(axis))]
    return lax.ppermute(value, axis, pairs)


def head_norm(heads_in, gain):
    return (
        heads_in * lax.rsqrt(jnp.mean(heads_in * heads_in, axis=-1, keepdims=True) + 1e-06) * gain
    )


def rotary(heads_in, positions):
    head_size = heads_in.shape[-1]
    blocks = (head_size // 8, 7 * head_size // 16, 7 * head_size // 16)
    pieces = []
    offset = 0
    for axis_id in range(3):
        width = blocks[axis_id]
        half = width // 2
        freq = 256.0 ** (-jnp.arange(half, dtype=jnp.float32) / half)
        angle = positions[axis_id].astype(jnp.float32)[:, None] * freq[None, :]
        cosine = jnp.cos(angle)[:, None, :]
        sine = jnp.sin(angle)[:, None, :]
        first = heads_in[..., offset : offset + half]
        second = heads_in[..., offset + half : offset + width]
        pieces.append(first * cosine - second * sine)
        pieces.append(second * cosine + first * sine)
        offset = offset + width
    return jnp.concatenate(pieces, axis=-1)


def local(latent, positions, text_kv, text_len, modulation, w_qkv, norm_gains, w_out, guidance):
    rows_here = latent.shape[0]
    width_dev = w_qkv.shape[2]
    heads_dev = width_dev // HEAD_DIM
    text_dev = text_kv.shape[2]
    branch = lax.axis_index("cfg")
    xfloat = latent.astype(jnp.float32)
    center = xfloat - jnp.mean(xfloat, axis=-1, keepdims=True)
    normed = center * lax.rsqrt(jnp.mean(center * center, axis=-1, keepdims=True) + 1e-06)
    both_mod = (
        normed[None] * (1.0 + modulation[1][:, None, :]) + modulation[0][:, None, :]
    ).astype(jnp.bfloat16)
    rows_w = w_qkv.shape[1]
    columns = lax.dynamic_slice_in_dim(both_mod, branch * rows_w, rows_w, 2)
    terms = jnp.einsum("btd,jde->bjte", columns, w_qkv, preferred_element_type=jnp.float32)
    projected = summed_on_arrival(terms.astype(jnp.bfloat16), "cfg", 0)[0]
    queries = rotary(
        head_norm(projected[0].reshape(rows_here, heads_dev, HEAD_DIM), norm_gains[0]), positions
    ).astype(jnp.bfloat16)
    keys = rotary(
        head_norm(projected[1].reshape(rows_here, heads_dev, HEAD_DIM), norm_gains[1]), positions
    ).astype(jnp.bfloat16)
    keys = keys.reshape(rows_here, width_dev)
    value_rows = projected[2].astype(jnp.bfloat16)
    text_raw = text_kv[0, 0].astype(jnp.float32).reshape(text_dev, heads_dev, HEAD_DIM)
    text_keys = head_norm(text_raw, norm_gains[1]).astype(jnp.bfloat16).reshape(text_dev, width_dev)
    text_values = text_kv[0, 1]
    length = text_len[0]
    scale = HEAD_DIM ** (-0.5)

    def attend(carry, key_rows, val_rows, valid):
        running_sum, accum = carry
        count = key_rows.shape[0]
        key_heads = key_rows.reshape(count, heads_dev, HEAD_DIM)
        val_heads = val_rows.reshape(count, heads_dev, HEAD_DIM)
        scores = (
            jnp.einsum("thd,nhd->htn", queries, key_heads, preferred_element_type=jnp.float32)
            * scale
        )
        expo = jnp.where(valid[None, None, :], jnp.exp(scores), 0.0)
        new_sum = running_sum + jnp.sum(expo, axis=-1)
        new_acc = accum + jnp.einsum(
            "htn,nhd->htd", expo.astype(jnp.bfloat16), val_heads, preferred_element_type=jnp.float32
        )
        return (new_sum, new_acc)

    start_state = (
        jnp.zeros((heads_dev, rows_here), jnp.float32),
        jnp.zeros((heads_dev, rows_here, HEAD_DIM), jnp.float32),
    )
    carry = start_state
    image_keys, image_values, prompt_keys, prompt_values = (
        *side_by_side((keys, value_rows), "seq", 0, 1),
        *side_by_side((text_keys, text_values), "seq", 0, 1),
    )
    carry = attend(carry, image_keys, image_values, jnp.ones((image_keys.shape[0],), bool))
    text_index = jnp.arange(prompt_keys.shape[0], dtype=jnp.int32)
    state = attend(carry, prompt_keys, prompt_values, text_index < length)
    final_sum, final_acc = state
    attended = (
        (final_acc / final_sum[..., None])
        .transpose(1, 0, 2)
        .reshape(rows_here, width_dev)
        .astype(jnp.bfloat16)
    )
    strength = guidance[0]
    half_cols = w_out.shape[1]
    full_out = lax.all_gather(w_out, "cfg", axis=1, tiled=True)
    summed = summed_on_arrival(
        jnp.dot(attended, full_out, preferred_element_type=jnp.float32).astype(jnp.bfloat16),
        "tensor",
        0,
    )
    gate = lax.dynamic_index_in_dim(modulation[2], branch, 0, keepdims=False)
    mine = (gate * summed).astype(jnp.bfloat16)
    own_half = lax.dynamic_slice_in_dim(mine, branch * half_cols, half_cols, 1)
    send_half = lax.dynamic_slice_in_dim(mine, (1 - branch) * half_cols, half_cols, 1)
    other = swapped(send_half, "cfg", 0)
    cond_rows = jnp.where(branch == 0, own_half, other).astype(jnp.float32)
    uncond_rows = jnp.where(branch == 0, other, own_half).astype(jnp.float32)
    guided = (uncond_rows + strength * (cond_rows - uncond_rows)).astype(jnp.bfloat16)
    return guided


def solution(mesh):
    placed = (
        P(("groups", "seq"), None),
        P(None, ("groups", "seq")),
        P("cfg", None, ("groups", "seq"), "tensor"),
        P(("groups", "cfg")),
        P(None, "groups", None),
        P(None, "cfg", "tensor"),
        P(),
        P("tensor", "cfg"),
        P("groups"),
    )
    return jax.shard_map(
        local,
        mesh=mesh,
        in_specs=placed,
        out_specs=P(("groups", "seq", "tensor"), "cfg"),
        check_vma=False,
    )
```

profile of v0, /device:TPU:33, one launch (start us, length us, event | category | flops | bytes accessed | tf_op | source)
XLA Modules:
  0.0 300.6 jit_solution(2850330878719103460)
XLA Ops:
  6.6 1.5 fusion.31
  8.1 1.7 convert_reduce_fusion.1
  9.8 2.0 fusion.9
  11.7 2.2 fusion.7
  14.0 1.5 constant_dynamic-slice_fusion.1
  15.5 7.1 %convert_bitcast_fusion = bf16[2,1,3,256,768]{4,3,2,1,0:T(8,128)(2,1)S(1)} fusion(bf16[3,1536,768]{2,1,0:T(8,128)(2,1)} %param.14, f32[2,1536]{1,0:T(2,128)S(1)} %get-tuple-element.50, f32[2,1536]{1,0:T(2,128)S(1)} %get-tuple-element.49, f32[256,1536]{1,0:T(8,128)S(1)} %constant_dynamic-slice_fusion.1), kind=kOutput, calls=%fused_computation.16 | convolution fusion | flops 3627417600 | bytes 11034624 | tf_op jit(solution)/shard_map/btd,jde->bjte/dot_general | solution.py:75
  22.6 25.7 %all_to_all.10 = bf16[2,1,3,256,768]{4,3,2,1,0:T(8,128)(2,1)S(1)} all-to-all(bf16[2,1,3,256,768]{4,3,2,1,0:T(8,128)(2,1)S(1)} %convert_bitcast_fusion), channel_id=1, replica_groups=mesh['groups'=2,'seq'=16,'tensor'=4,'cfg'=2] {'cfg'}, dimensions={0} | all-to-all | bytes 4718592 | tf_op jit(solution)/shard_map/all_to_all | solution.py:16
  48.3 0.4 convert_reduce_fusion
  48.7 0.1 fusion.29
  48.8 0.3 copy.37
  49.1 0.3 copy.38
  49.5 0.3 copy.41
  49.8 0.3 copy.42
  50.2 0.1 multiply_cosine_fusion.2
  50.3 0.1 copy.40
  50.4 0.1 copy.39
  50.6 0.3 multiply_multiply_fusion.1
  50.9 0.3 multiply_multiply_fusion
  51.1 1.0 multiply_cosine_fusion
  52.1 0.6 add_convert_fusion.6
  52.7 1.9 add_convert_fusion.1
  54.6 3.3 %concatenate.15 = bf16[256,6,128]{2,0,1:T(8,128)(2,1)} concatenate(bf16[256,6,8]{2,0,1:T(8,128)(2,1)S(1)} %get-tuple-element.27, bf16[256,6,8]{2,0,1:T(8,128)(2,1)S(1)} %get-tuple-element.28, bf16[256,6,28]{2,0,1:T(8,128)(2,1)} %get-tuple-element.25, bf16[256,6,28]{2,0,1:T(8,128)(2,1)} %get-tuple-element.26, bf16[256,6,28]{2,0,1:T(8,128)(2,1)} %get-tuple-element.16, ...), dimensions={2} | concatenate | bytes 786432 | tf_op jit(solution)/shard_map/concatenate | solution.py:58
  58.0 1.2 copy.43
  59.1 0.2 copy.44
  59.3 1.0 pad_maximum_fusion
  60.4 0.7 all-gather.5.cloned.1.call-update
  61.2 2.6 add_convert_fusion.4
  63.8 0.1 reduce_sum.89
  63.9 0.1 mul.443
  64.0 36.4 %all_gather.10 = bf16[256,1536]{1,0:T(8,128)(2,1)S(1)} all-gather(bf16[16,1536]{1,0:T(8,128)(2,1)S(1)} %pad_maximum_fusion.1), channel_id=1, replica_groups=mesh['groups'=2,'seq'=16,'tensor'=4,'cfg'=2] {'seq'}, dimensions={0}, use_global_device_ids=true | all-gather | bytes 835584 | tf_op jit(solution)/shard_map/all_gather | solution.py:26
  100.5 0.9 copy.50
  101.5 0.2 copy.48
  102.3 2.5 concatenate.14
  104.8 0.6 fusion.32
  105.3 102.6 %all-gather.3.cloned.1.call-done = bf16[4096,1536]{1,0:T(8,128)(2,1)} async-done(((bf16[256,1536]{1,0:T(8,128)(2,1)}), bf16[4096,1536]{1,0:T(8,128)(2,1)}) %all-gather.3.cloned.1.call-update) | async-done | bytes 12582928 | tf_op jit(solution)/shard_map/all_gather | solution.py:26
  207.9 10.3 %fusion.28 = (bf16[4096,768]{1,0:T(8,128)(2,1)}, bf16[4096,768]{1,0:T(8,128)(2,1)}) fusion(bf16[4096,1536]{1,0:T(8,128)(2,1)} %all-gather.3.cloned.1.call-done), kind=kLoop, calls=%fused_computation.87 | loop fusion | bytes 25165824 | tf_op jit(solution)/shard_map/split | solution.py:26
  218.2 8.9 %copy.47 = bf16[4096,768]{0,1:T(8,128)(2,1)} copy(bf16[4096,768]{1,0:T(8,128)(2,1)} %get-tuple-element.6) | data formatting | bytes 12582912 | tf_op jit(solution)/shard_map/split | solution.py:26
  227.1 8.8 %copy.45 = bf16[4096,768]{0,1:T(8,128)(2,1)} copy(bf16[4096,768]{1,0:T(8,128)(2,1)} %get-tuple-element.5) | data formatting | bytes 12582912 | tf_op jit(solution)/shard_map/split | solution.py:26
  235.9 13.8 %fusion = (f32[6,256]{1,0:T(8,128)S(1)}, f32[6,256,4096]{2,1,0:T(8,128)}) fusion(bf16[256,6,128]{2,0,1:T(8,128)(2,1)S(1)} %concatenate.14, bf16[4096,6,128]{0,2,1:T(8,128)(2,1)} %bitcast.84), kind=kOutput, calls=%fused_computation.1 | convolution fusion | flops 1623194112 | bytes 31856640 | tf_op jit(solution)/shard_map/thd,nhd->htn/dot_general | solution.py:97
  249.7 10.4 %fusion.2 = f32[6,256,128]{1,2,0:T(8,128)S(1)} fusion(bf16[4096,6,128]{0,2,1:T(8,128)(2,1)S(1)} %bitcast.83, f32[6,256,4096]{2,1,0:T(8,128)} %get-tuple-element.46), kind=kOutput, calls=%fused_computation.3 | convolution fusion | flops 1623195648 | bytes 32243712 | tf_op jit(solution)/shard_map/htn,nhd->htd/dot_general | solution.py:102
  260.2 0.3 fusion.19
  260.5 4.9 %convolution_convert_fusion = bf16[256,3072]{1,0:T(8,128)(2,1)} fusion(bf16[256,768]{0,1:T(8,128)(2,1)S(1)} %bitcast.92, bf16[768,3072]{1,0:T(8,128)(2,1)} %all-gather.5.cloned.1.call-done), kind=kOutput, calls=%fused_computation.10 | convolution fusion | flops 1208745984 | bytes 6684672 | tf_op jit(solution)/shard_map/dot_general | solution.py:130
  265.4 4.3 %all-to-all-start.1 = ((bf16[4,64,3072]{2,1,0:T(8,128)(2,1)}), bf16[4,64,3072]{2,1,0:T(8,128)(2,1)S(1)}, u32[]{:S(2)}, u32[]{:S(2)}) async-start(bf16[4,64,3072]{2,1,0:T(8,128)(2,1)} %bitcast.31), calls=%async_computation.1 | async-start | bytes 3145728 | tf_op jit(solution)/shard_map/all_to_all | solution.py:16
  269.7 19.8 %all-to-all-done.1 = bf16[4,64,3072]{2,1,0:T(8,128)(2,1)S(1)} async-done(((bf16[4,64,3072]{2,1,0:T(8,128)(2,1)}), bf16[4,64,3072]{2,1,0:T(8,128)(2,1)S(1)}, u32[]{:S(2)}, u32[]{:S(2)}) %all-to-all-start.1) | async-done | bytes 1572896 | tf_op jit(solution)/shard_map/all_to_all | solution.py:16
  289.5 0.2 convert_reduce_fusion.2
  289.9 2.0 collective-permute-start
  292.5 0.4 collective-permute-done
  292.9 0.8 fusion.22
  (50 shorter events, 0.7 us)
Async XLA Ops:
  6.5 5.2 %copy-start = (bf16[256,3072]{1,0:T(8,128)(2,1)S(1)}, bf16[256,3072]{1,0:T(8,128)(2,1)}, u32[]{:S(2)}) copy-start(bf16[256,3072]{1,0:T(8,128)(2,1)} %param.9) | copy-start | bytes 4718596
  6.5 201.3 %all-gather.3.cloned.1.call-start = ((), (), s32[]{:S(2)}) async-start(), calls=%async_computation.2 | async-start | bytes 13369344 | tf_op jit(solution)/shard_map/all_gather | solution.py:26
  49.1 1.0 copy-start.7
  49.1 1.0 copy-start.6
  52.1 2.5 copy-start.1
  52.1 2.5 copy-start.2
  60.4 200.1 %all-gather.5.cloned.1.call-start = ((), (), s32[]{:S(2)}) async-start(), calls=%async_computation.3 | async-start | bytes 7077888 | tf_op jit(solution)/shard_map/all_gather | solution.py:128
  61.2 2.6 copy-start.4
  235.9 13.8 %slice-start = ((s8[6291456]{0:T(1024)(128)(4,1)}), s8[4194304]{0:T(1024)(128)(4,1)S(1)}, s32[]{:S(2)}) async-start(s8[6291456]{0:T(1024)(128)(4,1)} %bitcast.81), calls=%async_computation.4 | async-start | bytes 8388608
  235.9 13.8 %slice-start.1 = ((s8[6291456]{0:T(1024)(128)(4,1)}), s8[2097152]{0:T(1024)(128)(4,1)S(1)}, s32[]{:S(2)}) async-start(s8[6291456]{0:T(1024)(128)(4,1)} %bitcast.81), calls=%async_computation.5 | async-start | bytes 4194304
  249.7 10.4 %copy-start.3 = (bf16[256,768]{0,1:T(8,128)(2,1)S(1)}, bf16[256,768]{0,1:T(8,128)(2,1)}, u32[]{:S(2)}) copy-start(bf16[256,768]{0,1:T(8,128)(2,1)} %copy.50) | copy-start | bytes 1179652
  265.4 4.3 %copy-start.5 = (f32[1,2,3072]{2,1,0:T(2,128)S(1)}, f32[1,2,3072]{2,1,0:T(2,128)}, u32[]{:S(2)}) copy-start(f32[1,2,3072]{2,1,0:T(2,128)} %get-tuple-element.29) | copy-start | bytes 73732
  265.4 24.1 %all-to-all-start.1 = ((bf16[4,64,3072]{2,1,0:T(8,128)(2,1)}), bf16[4,64,3072]{2,1,0:T(8,128)(2,1)S(1)}, u32[]{:S(2)}, u32[]{:S(2)}) async-start(bf16[4,64,3072]{2,1,0:T(8,128)(2,1)} %bitcast.31), calls=%async_computation.1 | async-start | bytes 3145728 | tf_op jit(solution)/shard_map/all_to_all | solution.py:16
  289.9 3.1 %collective-permute-start = (bf16[64,1536]{1,0:T(8,128)(2,1)S(1)}, bf16[64,1536]{1,0:T(8,128)(2,1)S(1)}, u32[]{:S(2)}, u32[]{:S(2)}) collective-permute-start(bf16[64,1536]{1,0:T(8,128)(2,1)S(1)} %constant_dynamic-slice_fusion.2), channel_id=1, source_target_pairs={{0,1},{1,0},{2,3},{3,2},{4,5},{5,4},{6,7},{7,6},{8,9},{9,8},{10,11... | collective-permute-start | bytes 589832 | tf_op jit(solution)/shard_map/ppermute | solution.py:32
Sparse Core Ops, SparseCore 0:
  60.5 147.3 all-gather.2
  209.7 20.5 all-gather.4
where the time goes:
time: 302 us; the launch traced here: 301 us
  waiting for transfers between devices  124 us (41%)
  blocking collectives  62.1 us (21%)
  local copies, waits for them, and re-layouts  39.5 us (13%)
  matrix products  37 us (12%)
  other arithmetic  16.9 us (6%)
  between operations  15.1 us (5%)
  starting transfers between devices  6.39 us (2%)
    all_gather x1, waiting for transfers between devices, side_by_side(): lax.all_gather(both, axis, axis=dim, tiled=True)  103 us
    all_gather x1, blocking collectives, side_by_side(): lax.all_gather(both, axis, axis=dim, tiled=True)  36.4 us
    split x6, local copies, waits for them, and re-layouts, side_by_side(): jnp.split(lax.all_gather(both, axis, axis=dim, tiled=True), ends, axis=al...  29.2 us
    all_to_all x1, blocking collectives, summed_on_arrival(): lax.all_to_all(in_blocks(shard, dim, devices), axis, 0, 0, tiled=True)  25.7 us
    all_to_all x1, waiting for transfers between devices, summed_on_arrival(): lax.all_to_all(in_blocks(shard, dim, devices), axis, 0, 0, tiled=True)  19.8 us
    dot_general x2, matrix products, attend(): jnp.einsum('thd,nhd->htn', queries, key_heads, preferred_element_type=jnp...  14.3 us
    dot_general x2, matrix products, attend(): jnp.einsum('htn,nhd->htd', expo.astype(jnp.bfloat16), val_heads, preferre...  10.7 us
    dot_general x1, matrix products, local(): jnp.einsum('btd,jde->bjte', columns, w_qkv, preferred_element_type=jnp.fl...  7.06 us
  transfers between devices with their start and end apart: 4, of which 3 were waited for; matrix products, arithmetic and copies ran while one was open for 20% of the time, Pallas kernels for 0%

commit v1 on v0

v1 whole, which is shorter than its diff:
```python
import functools

import jax
import jax.numpy as jnp
import numpy as np
from jax import lax
from jax.experimental import pallas as pl
from jax.experimental.pallas import tpu as pltpu
from jax.sharding import PartitionSpec as P

HEAD_DIM = 128
MESH = pl.DeviceIdType.MESH
F32 = jnp.float32
BF16 = jnp.bfloat16
STARTS = (0, 40, 96)
LIMITS = (33, 45, 80)
TABLE_ROWS = 256
BLOCKS = (16, 56, 56)


def rotary_table():
    table = np.zeros((TABLE_ROWS, 2 * HEAD_DIM), np.float32)
    offset = 0
    for start, limit, width in zip(STARTS, LIMITS, BLOCKS):
        half = width // 2
        freq = (256.0 ** (-np.arange(half, dtype=np.float64) / half)).astype(np.float32)
        angle = np.arange(limit, dtype=np.float32)[:, None] * freq[None, :]
        cosine, sine = np.cos(angle.astype(np.float64)), np.sin(angle.astype(np.float64))
        rows = slice(start, start + limit)
        table[rows, offset : offset + half] = cosine
        table[rows, offset + half : offset + width] = cosine
        table[rows, HEAD_DIM + offset : HEAD_DIM + offset + half] = -sine
        table[rows, HEAD_DIM + offset + half : HEAD_DIM + offset + width] = sine
        offset += width
    high = jnp.asarray(table).astype(BF16)
    low = (jnp.asarray(table) - high.astype(F32)).astype(BF16)
    return jnp.concatenate([high, low], axis=0)


def partner_lanes(x):
    lane = lax.broadcasted_iota(jnp.int32, x.shape, 1)
    small, large = BLOCKS[0] // 2, BLOCKS[1] // 2
    wide_first = ((lane >= 16) & (lane < 44)) | ((lane >= 72) & (lane < 100))
    wide = jnp.where(
        wide_first, pltpu.roll(x, HEAD_DIM - large, 1), pltpu.roll(x, large, 1)
    )
    narrow = jnp.where(lane < small, pltpu.roll(x, HEAD_DIM - small, 1), pltpu.roll(x, small, 1))
    return jnp.where(lane < 2 * small, narrow, wide)


def contract_first(a, b):
    return lax.dot_general(a, b, (((0,), (0,)), ((), ())), preferred_element_type=F32)


def contract_last(a, b):
    return lax.dot_general(a, b, (((1,), (1,)), ((), ())), preferred_element_type=F32)


def kernel(
    sizes,
    latent,
    positions,
    text_kv,
    text_len,
    modulation,
    w_qkv,
    gains,
    w_out,
    guidance,
    table,
    out,
    X,
    W,
    WO,
    T,
    A,
    Q,
    CT,
    ST,
    cs,
    bw,
    acc,
    lsum,
    KV,
    att,
    PO,
    G,
    RB,
    local_sem,
    zs,
    zr,
    xs,
    xr,
    dzs,
    dzr,
    dxs,
    dxr,
    ts,
    tr,
    As,
    Ar,
    wsend,
    wrecv,
    asend,
    arecv,
    gs,
    gr,
):
    n_seq, n_ten = sizes
    c = lax.axis_index("cfg")
    z = lax.axis_index("seq")
    x = lax.axis_index("tensor")
    par = lax.rem(x, 2)
    rows, d = latent.shape
    width = w_qkv.shape[2]
    heads = width // HEAD_DIM
    kdev = w_qkv.shape[1]
    half = rows // 2
    ch = half // 4
    own = n_seq - 1
    opp = n_seq - 2
    last_step = n_seq // 2
    n_ev = 4 * (last_step - 1) + 2
    first_last = 4 * (last_step - 1)
    z_up = lax.rem(z + 1, n_seq)
    z_down = lax.rem(z + n_seq - 1, n_seq)
    z_next = lax.rem(z + 1 - 2 * c + n_seq, n_seq)
    scale = HEAD_DIM**-0.5 * 1.4426950408889634

    def local(src, dst, k):
        return pltpu.make_async_copy(src, dst, local_sem.at[k])

    def remote(src, dst, ssem, rsem, device):
        return pltpu.make_async_remote_copy(
            src_ref=src,
            dst_ref=dst,
            send_sem=ssem,
            recv_sem=rsem,
            device_id=device,
            device_id_type=MESH,
        )

    mine_k = pl.ds(pl.multiple_of(c * kdev, kdev), kdev)
    other_k = pl.ds(pl.multiple_of((1 - c) * kdev, kdev), kdev)
    for j in range(3):
        local(w_qkv.at[j], W.at[j, mine_k], j).start()
    local(latent, X.at[own], 3).start()
    local(text_kv.at[0], T.at[own], 4).start()
    local(w_out, WO, 5).start()

    barrier = pltpu.get_barrier_semaphore()
    peers = [
        {"cfg": 1 - c},
        {"seq": z_up},
        {"seq": z_down},
        *({"tensor": lax.rem(x + k, n_ten)} for k in range(1, n_ten)),
    ]
    for peer in peers:
        pl.semaphore_signal(barrier, inc=1, device_id=peer, device_id_type=MESH)
    pl.semaphore_wait(barrier, len(peers))

    def chunk(e, core):
        is_last = e >= first_last
        idx = jnp.where(is_last, opp, 2 * lax.div(e, 4) + core)
        j = jnp.where(is_last, 2 * core + e - first_last, lax.rem(e, 4))
        return idx, j

    def row_of(j, parity):
        return pl.multiple_of(parity * half + j * ch, ch)

    def z_copy(src, idx, j, e):
        return remote(
            src,
            X.at[idx, pl.ds(row_of(j, par), ch)],
            zs.at[e],
            zr.at[e],
            {"seq": z_next},
        )

    def x_copy(e, parity):
        idx, j = chunk(e, c)
        back = jnp.where(e >= first_last, e - first_last, lax.div(j, 2))
        ref = X.at[idx, pl.ds(row_of(j, parity), ch)]
        to = lax.rem(x + 1 - 2 * back + n_ten, n_ten)
        return remote(ref, ref, xs.at[e], xr.at[e], {"tensor": to})

    def d_copy(e, core, parity, ssem, rsem):
        idx, j = chunk(e, core)
        ref = X.at[idx, pl.ds(row_of(j, parity), ch)]
        return remote(ref, ref, ssem.at[e], rsem.at[e], {"cfg": 1 - c})

    def z_event(e):
        idx, j = chunk(e, c)
        here = X.at[idx, pl.ds(row_of(j, par), ch)]
        z_copy(here, idx, j, e).wait_recv()
        going = (e < first_last - 4) | ((e < first_last) & (lax.div(j, 2) == c))

        @pl.when(going)
        def _():
            far = e >= first_last - 4
            ne = jnp.where(far, first_last + j - 2 * c, e + 4)
            nidx = jnp.where(far, opp, idx + 2)
            z_copy(here, nidx, j, ne).start()

        x_copy(e, par).start()
        d_copy(e, c, par, dzs, dzr).start()

    def x_event(e):
        x_copy(e, 1 - par).wait_recv()
        d_copy(e, c, 1 - par, dxs, dxr).start()

    def event(e):
        @pl.when(e < n_ev)
        def _():
            z_event(e)

        @pl.when((e >= 2) & (e < n_ev + 2))
        def _():
            x_event(e - 2)

    def t_copies(src, idx, direction):
        to = {"seq": z_down if direction else z_up}
        return (
            remote(T.at[src], T.at[idx], ts.at[idx], tr.at[idx], to),
            remote(A.at[src], A.at[idx], As.at[idx], Ar.at[idx], to),
        )

    def text_event(u):
        for direction in range(2):

            @pl.when((u < last_step) | (direction == 0))
            def _():
                idx = jnp.where(u < last_step, 2 * (u - 1) + direction, opp)
                for copy in t_copies(idx, idx, direction):
                    copy.wait_recv()

                @pl.when((u < last_step - 1) | ((u == last_step - 1) & (direction == 0)))
                def _():
                    nxt = jnp.where(u < last_step - 1, idx + 2, opp)
                    for copy in t_copies(idx, nxt, direction):
                        copy.start()

    for j in range(4):
        z_copy(latent.at[pl.ds(row_of(j, par), ch)], c, j, j).start()
    w_copies = [
        remote(w_qkv.at[j], W.at[j, mine_k], wsend.at[j], wrecv.at[j], {"cfg": 1 - c})
        for j in range(3)
    ]
    w_copies[2].start()
    local(text_kv.at[0], T.at[own], 4).wait()
    t_copies(own, 0, 0)[0].start()
    t_copies(own, 1, 1)[0].start()
    w_copies[1].start()
    w_copies[0].start()

    local(latent, X.at[own], 3).wait()
    xf = X[own].astype(F32)
    mean = jnp.mean(xf, axis=-1, keepdims=True)
    center = xf - mean
    rstd = lax.rsqrt(jnp.mean(center * center, axis=-1, keepdims=True) + 1e-06)
    lane = lax.broadcasted_iota(jnp.int32, (rows, HEAD_DIM), 1)
    stats = jnp.where(lane == 3, mean, jnp.where(lane == 4, rstd, 0.0))
    stats = jnp.transpose(stats)[0:8]
    sub = lax.broadcasted_iota(jnp.int32, (8, rows), 0)
    pos = positions[...].astype(F32)
    for k in range(3):
        stats = jnp.where(sub == k, pos[k : k + 1], stats)
    A[own] = stats
    t_copies(own, 0, 0)[1].start()
    t_copies(own, 1, 1)[1].start()

    kt = 256

    def fold(j, part):
        def body(i, carry):
            base = pl.multiple_of(part * kdev + i * kt, kt)
            shift_row = modulation[0, pl.ds(c, 1), pl.ds(base, kt)]
            scale_row = modulation[1, pl.ds(c, 1), pl.ds(base, kt)]
            srow = lax.broadcasted_iota(jnp.int32, (8, kt), 0)
            both = jnp.where(srow == 0, 1.0 + scale_row, jnp.where(srow == 1, shift_row, 0.0))
            cols = jnp.transpose(both)
            raw = W[j, pl.ds(base, kt), :].astype(F32)
            new = (raw * cols[:, 0:1]).astype(BF16)
            W[j, pl.ds(base, kt), :] = new
            cs[j] += jnp.sum(new.astype(F32).reshape(kt // 8, 8, width), axis=0)
            bw[j] += jnp.sum((raw * cols[:, 1:2]).reshape(kt // 8, 8, width), axis=0)
            return carry

        lax.fori_loop(0, kdev // kt, body, 0)

    def finish(j):
        cs[j] = jnp.broadcast_to(jnp.sum(cs[j], axis=0, keepdims=True), (8, width))
        bw[j] = jnp.broadcast_to(jnp.sum(bw[j], axis=0, keepdims=True), (8, width))

    cs[...] = jnp.zeros_like(cs)
    bw[...] = jnp.zeros_like(bw)
    acc[...] = jnp.zeros_like(acc)
    lsum[...] = jnp.zeros_like(lsum)
    for j in (2, 1, 0):
        local(w_qkv.at[j], W.at[j, mine_k], j).wait()
        fold(j, c)

    def w_arrive(j):
        remote(w_qkv.at[j], W.at[j, other_k], wsend.at[j], wrecv.at[j], {"cfg": 1 - c}).wait_recv()
        fold(j, 1 - c)
        finish(j)

    def tables(idx, at):
        a = A[idx]
        cols = jnp.transpose(a)
        at_rows = pl.ds(at, rows)
        rs = cols[:, 4:5]
        ST[0, at_rows] = jnp.broadcast_to(rs, (rows, HEAD_DIM))
        ST[1, at_rows] = jnp.broadcast_to(cols[:, 3:4] * rs, (rows, HEAD_DIM))
        index = lax.broadcasted_iota(jnp.int32, (TABLE_ROWS, rows), 0).astype(F32)
        hot = (
            (index == a[0:1] + float(STARTS[0]))
            | (index == a[1:2] + float(STARTS[1]))
            | (index == a[2:3] + float(STARTS[2]))
        )
        hot = jnp.where(hot, 1.0, 0.0).astype(BF16)
        CT[at_rows] = contract_first(hot, table[0:TABLE_ROWS]) + contract_first(
            hot, table[TABLE_ROWS : 2 * TABLE_ROWS]
        )

    def affine(block, j, lanes, m):
        return block * ST[0, 0:m] - ST[1, 0:m] * cs[j, 0:1, lanes] + bw[j, 0:1, lanes]

    def head_rows(block, j, lanes, m, gain):
        v = affine(block, j, lanes, m)
        r = lax.rsqrt(jnp.mean(v * v, axis=-1, keepdims=True) + 1e-06)
        v = v * gain
        v = v * CT[0:m, 0:HEAD_DIM] + partner_lanes(v) * CT[0:m, HEAD_DIM : 2 * HEAD_DIM]
        return (v * r).astype(BF16)

    q_gain = gains[0:1, :]
    k_gain = gains[1:2, :]

    def attend(h, keys, values, m, mask=None):
        s = contract_last(Q[h], keys)
        p = jnp.exp2(s * scale)
        if mask is not None:
            p = jnp.where(mask, p, 0.0)
        part = p[:, 0:HEAD_DIM]
        for k in range(1, m // HEAD_DIM):
            part = part + p[:, k * HEAD_DIM : (k + 1) * HEAD_DIM]
        lsum[h] += part
        acc[h] += jnp.dot(p.astype(BF16), values, preferred_element_type=F32)

    pair = 2 * HEAD_DIM

    def key_values(load, t, m):
        wide = slice(t * pair, (t + 1) * pair)
        k2 = jnp.dot(load(), W[1, :, wide], preferred_element_type=F32)
        v2 = jnp.dot(load(), W[2, :, wide], preferred_element_type=F32)
        for hh in range(2):
            h = 2 * t + hh
            lanes = slice(h * HEAD_DIM, (h + 1) * HEAD_DIM)
            sub_l = slice(hh * HEAD_DIM, (hh + 1) * HEAD_DIM)
            keys = head_rows(k2[:, sub_l], 1, lanes, m, k_gain)
            values = affine(v2[:, sub_l], 2, lanes, m).astype(BF16)
            attend(h, keys, values, m)

    event(0)
    w_arrive(2)
    tables(own, 0)
    event(1)
    text_event(1)
    w_arrive(1)
    event(2)
    w_arrive(0)
    event(3)
    for t in range(heads // 2):
        wide = slice(t * pair, (t + 1) * pair)
        q2 = jnp.dot(X[own], W[0, :, wide], preferred_element_type=F32)
        for hh in range(2):
            h = 2 * t + hh
            lanes = slice(h * HEAD_DIM, (h + 1) * HEAD_DIM)
            Q[h] = head_rows(
                q2[:, hh * HEAD_DIM : (hh + 1) * HEAD_DIM], 0, lanes, rows, q_gain
            )
    event(4)
    for t in range(heads // 2):
        key_values(lambda: X[own], t, rows)
    event(5)

    def wait_partner(e):
        d_copy(e, 1 - c, par, dzs, dzr).wait_recv()
        d_copy(e, 1 - c, 1 - par, dxs, dxr).wait_recv()

    def step(s, carry):
        def waits(k, carry):
            wait_partner(4 * (s - 1) + k)
            return carry

        lax.fori_loop(0, 4, waits, 0)
        base = pl.multiple_of(2 * (s - 1), 2)
        tables(base, 0)
        tables(base + 1, rows)
        for t in range(heads // 2):
            key_values(lambda: X[pl.ds(base, 2)].reshape(2 * rows, d), t, 2 * rows)
            event(4 * s + 2 + t)
        text_event(s + 1)
        event(4 * s + 5)
        return carry

    lax.fori_loop(1, last_step, step, 0)

    key_lane = lax.broadcasted_iota(jnp.int32, (1, n_seq * T.shape[2]), 1)
    trows = T.shape[2]
    slot = lax.div(key_lane, trows)
    away = lax.div(slot, 2) + 1
    sign = 1 - 2 * lax.rem(slot, 2)
    plane = lax.rem(z - sign * away + 2 * n_seq, n_seq)
    plane = jnp.where(slot == own, z, plane)
    plane = jnp.where(slot == opp, lax.rem(z + last_step, n_seq), plane)
    used = plane * trows + lax.rem(key_lane, trows) < text_len[0]
    m_text = n_seq * trows
    for h in range(heads):
        lanes = slice(h * HEAD_DIM, (h + 1) * HEAD_DIM)
        tk = T[:, 0, :, lanes].reshape(m_text, HEAD_DIM).astype(F32)
        r = lax.rsqrt(jnp.mean(tk * tk, axis=-1, keepdims=True) + 1e-06)
        keys = (tk * r * k_gain).astype(BF16)
        attend(h, keys, T[:, 1, :, lanes].reshape(m_text, HEAD_DIM), m_text, used)

    wait_partner(first_last)
    wait_partner(first_last + 1)
    tables(opp, 0)
    for t in range(heads // 2):
        key_values(lambda: X[opp], t, rows)

    for h in range(heads):
        total = jnp.sum(lsum[h], axis=-1, keepdims=True)
        att[0, :, h * HEAD_DIM : (h + 1) * HEAD_DIM] = (acc[h] / total).astype(BF16)
    swap = remote(att.at[0], att.at[1], asend.at[0], arecv.at[0], {"cfg": 1 - c})
    swap.start()
    local(w_out, WO, 5).wait()
    ocols = w_out.shape[1]
    mine_o = pl.multiple_of(c * ocols, ocols)
    nt = ocols // 3
    strength = guidance[0]
    cf = c.astype(F32)
    weight_own = strength * (1.0 - cf) + (1.0 - strength) * cf
    weight_other = 1.0 - weight_own
    for k in range(3):
        cols = slice(k * nt, (k + 1) * nt)
        PO[:, cols] = jnp.dot(att[0], WO[:, cols], preferred_element_type=F32)
    swap.wait()

    def g_copy(k, t):
        to = lax.rem(x + k, n_ten)
        qrows = rows // n_ten
        return remote(
            G.at[pl.ds(pl.multiple_of(to * qrows, qrows), qrows), pl.ds(t * nt, nt)],
            RB.at[k - 1, :, pl.ds(t * nt, nt)],
            gs.at[(k - 1) * 3 + t],
            gr.at[(k - 1) * 3 + t],
            {"tensor": to},
        )

    for t in range(3):
        cols = slice(t * nt, (t + 1) * nt)
        gate_own = modulation[2, pl.ds(c, 1), pl.ds(mine_o + t * nt, nt)]
        gate_other = modulation[2, pl.ds(1 - c, 1), pl.ds(mine_o + t * nt, nt)]
        other = jnp.dot(att[1], WO[:, cols], preferred_element_type=F32)
        G[:, cols] = (
            PO[:, cols] * (gate_own * weight_own) + other * (gate_other * weight_other)
        ).astype(BF16)
        for k in (2, 1, 3):
            g_copy(k, t).start()

    qrows = rows // n_ten
    for t in range(3):
        cols = slice(t * nt, (t + 1) * nt)
        total = G[pl.ds(pl.multiple_of(x * qrows, qrows), qrows), cols].astype(F32)
        for k in (1, 3, 2):
            g_copy(k, t).wait_recv()
            total = total + RB[k - 1, :, cols].astype(F32)
        out[:, cols] = total.astype(BF16)

    for t in range(3):
        for k in (1, 2, 3):
            g_copy(k, t).wait_send()
    for j in range(3):
        w_copies[j].wait_send()

    def sent(e, carry):
        x_copy(e, par).wait_send()
        d_copy(e, c, par, dzs, dzr).wait_send()
        d_copy(e, c, 1 - par, dxs, dxr).wait_send()
        idx, j = chunk(e, c)
        z_copy(X.at[idx, pl.ds(row_of(j, par), ch)], idx, j, e).wait_send()
        return carry

    lax.fori_loop(0, n_ev, sent, 0)

    def sent_text(idx, carry):
        for copy in t_copies(idx, idx, 0):
            copy.wait_send()
        return carry

    lax.fori_loop(0, own, sent_text, 0)


def solution(mesh):
    n_seq, n_ten = mesh.shape["seq"], mesh.shape["tensor"]

    def local(latent, positions, text_kv, text_len, modulation, w_qkv, gains, w_out, guidance):
        rows, d = latent.shape
        width = w_qkv.shape[2]
        heads = width // HEAD_DIM
        ocols = w_out.shape[1]
        n_ev = 4 * (n_seq // 2 - 1) + 2
        vmem, smem, anyw = pltpu.VMEM, pltpu.SMEM, pl.ANY
        spec = lambda space: pl.BlockSpec(memory_space=space)
        dma = pltpu.SemaphoreType.DMA
        return pl.pallas_call(
            functools.partial(kernel, (n_seq, n_ten)),
            out_shape=jax.ShapeDtypeStruct((rows // n_ten, ocols), BF16),
            in_specs=[
                spec(anyw),
                spec(vmem),
                spec(anyw),
                spec(smem),
                spec(vmem),
                spec(anyw),
                spec(vmem),
                spec(anyw),
                spec(smem),
                spec(vmem),
            ],
            out_specs=spec(vmem),
            scratch_shapes=[
                vmem((n_seq, rows, d), BF16),
                vmem((3, d, width), BF16),
                vmem((width, ocols), BF16),
                vmem((n_seq, 2, text_kv.shape[2], width), BF16),
                vmem((n_seq, 8, rows), F32),
                vmem((heads, rows, HEAD_DIM), BF16),
                vmem((2 * rows, 2 * HEAD_DIM), F32),
                vmem((2, 2 * rows, HEAD_DIM), F32),
                vmem((3, 8, width), F32),
                vmem((3, 8, width), F32),
                vmem((heads, rows, HEAD_DIM), F32),
                vmem((heads, rows, HEAD_DIM), F32),
                vmem((8, 128), F32),
                vmem((2, rows, width), BF16),
                vmem((rows, ocols), F32),
                vmem((rows, ocols), BF16),
                vmem((n_ten - 1, rows // n_ten, ocols), BF16),
                dma((6,)),
                dma((n_ev,)),
                dma((n_ev,)),
                dma((n_ev,)),
                dma((n_ev,)),
                dma((n_ev,)),
                dma((n_ev,)),
                dma((n_ev,)),
                dma((n_ev,)),
                dma((n_seq,)),
                dma((n_seq,)),
                dma((n_seq,)),
                dma((n_seq,)),
                dma((3,)),
                dma((3,)),
                dma((1,)),
                dma((1,)),
                dma((9,)),
                dma((9,)),
            ],
            compiler_params=pltpu.CompilerParams(
                collective_id=0, has_side_effects=True, vmem_limit_bytes=62 * 1024 * 1024
            ),
        )(
            latent,
            positions,
            text_kv,
            text_len,
            modulation,
            w_qkv,
            gains,
            w_out,
            guidance,
            rotary_table(),
        )

    placed = (
        P(("groups", "seq"), None),
        P(None, ("groups", "seq")),
        P("cfg", None, ("groups", "seq"), "tensor"),
        P(("groups", "cfg")),
        P(None, "groups", None),
        P(None, "cfg", "tensor"),
        P(),
        P("tensor", "cfg"),
        P("groups"),
    )
    return jax.shard_map(
        local,
        mesh=mesh,
        in_specs=placed,
        out_specs=P(("groups", "seq", "tensor"), "cfg"),
        check_vma=False,
    )
```

time: 302 us -> 190 us (0.63)
  Pallas kernels: 0 us -> 187 us
  waiting for transfers between devices: 124 us -> 0 us
  blocking collectives: 62.1 us -> 0 us
  local copies, waits for them, and re-layouts: 39.5 us -> 1.62 us
  matrix products: 37 us -> 0 us
  other arithmetic: 16.9 us -> 0 us
  between operations: 15.1 us -> 1.31 us
  starting transfers between devices: 6.39 us -> 0 us
    pallas_call x0 -> x1, Pallas kernels: none -> 187 us  [local(): pl.pallas_call(functools.partial(kernel, (n_seq, n_ten)), out_shape=jax.S...]
    all_gather x2 -> x0, waiting for transfers between devices: 103 us -> none  [the longest x1 103 us: side_by_side(): lax.all_gather(both, axis, axis=dim, tiled=True)]
    dot_general x6 -> x0, matrix products: 37 us -> none  [the longest x2 14.3 us: attend(): jnp.einsum('thd,nhd->htn', queries, key_heads, preferred_element_type=jnp...]
    all_gather x1 -> x0, blocking collectives: 36.4 us -> none  [side_by_side(): lax.all_gather(both, axis, axis=dim, tiled=True)]
    split x6 -> x0, local copies, waits for them, and re-layouts: 29.2 us -> none  [side_by_side(): jnp.split(lax.all_gather(both, axis, axis=dim, tiled=True), ends, axis=al...]
    all_to_all x1 -> x0, blocking collectives: 25.7 us -> none  [summed_on_arrival(): lax.all_to_all(in_blocks(shard, dim, devices), axis, 0, 0, tiled=True)]
    all_to_all x1 -> x0, waiting for transfers between devices: 19.8 us -> none  [summed_on_arrival(): lax.all_to_all(in_blocks(shard, dim, devices), axis, 0, 0, tiled=True)]
    concatenate x3 -> x0, local copies, waits for them, and re-layouts: 6.97 us -> none  [rotary(): return jnp.concatenate(pieces, axis=-1)]
  transfers between devices with their start and end apart: 4 -> 0, of which waited for: 3 -> 0; matrix products, arithmetic and copies ran while one was open for 20% -> 0% of each run, Pallas kernels for 0% -> 0%
where the time goes in v1:
time: 190 us
  Pallas kernels  187 us (98%)
    pallas_call x1, Pallas kernels, local(): pl.pallas_call(functools.partial(kernel, (n_seq, n_ten)), out_shape=jax.S...  187 us

profile of v1, /device:TPU:33, one launch (start us, length us, event | category | flops | bytes accessed | tf_op | source)
XLA Modules:
  0.0 190.2 jit_solution(3632428677957654561)
XLA Ops:
  1.3 187.2 %shard_map.100 = bf16[64,1536]{1,0:T(8,128)(2,1)} custom-call(bf16[256,3072]{1,0:T(8,128)(2,1)} %latent.1, s32[3,256]{1,0:T(4,128)} %positions.1, bf16[1,2,16,768]{3,2,1,0:T(8,128)(2,1)} %text_kv.1, s32[1]{0:T(128)S(6)} %copy.12.text_len, f32[3,2,3072]{2,1,0:T(2,128)} %modulation.1, bf16[3,1536,768]{2,1,0:T(8,128)(2,1)} %w_qkv.1, f32[2,128]{1,0:T(2,128)} %gains.1, ...), custom_call_target="tpu_custom_call" | custom-call | tf_op jit(solution)/shard_map/pallas_call | solution.py:517
  188.5 1.6 copy.14

commit v2 on v1

--- a/solution.py
+++ b/solution.py
@@ -70,6 +70,7 @@
     table,
     out,
     X,
+    XO,
     W,
     WO,
     T,
@@ -82,6 +83,7 @@
     acc,
     lsum,
     KV,
+    OW,
     att,
     PO,
     G,
@@ -124,7 +126,6 @@
     first_last = 4 * (last_step - 1)
     z_up = lax.rem(z + 1, n_seq)
     z_down = lax.rem(z + n_seq - 1, n_seq)
-    z_next = lax.rem(z + 1 - 2 * c + n_seq, n_seq)
     scale = HEAD_DIM**-0.5 * 1.4426950408889634
 
     def local(src, dst, k):
@@ -142,11 +143,21 @@
 
     mine_k = pl.ds(pl.multiple_of(c * kdev, kdev), kdev)
     other_k = pl.ds(pl.multiple_of((1 - c) * kdev, kdev), kdev)
-    for j in range(3):
-        local(w_qkv.at[j], W.at[j, mine_k], j).start()
-    local(latent, X.at[own], 3).start()
-    local(text_kv.at[0], T.at[own], 4).start()
-    local(w_out, WO, 5).start()
+    pair = 2 * HEAD_DIM
+    pairs = width // pair
+
+    def w_from(t, j):
+        return w_qkv.at[j, :, pl.ds(t * pair, pair)]
+
+    def w_local(t, j):
+        return local(w_from(t, j), W.at[t, mine_k, pl.ds(j * pair, pair)], 3 + 3 * t + j)
+
+    local(latent, XO.at[pl.ds(0, rows)], 0).start()
+    local(text_kv.at[0], T.at[own], 1).start()
+    for t in range(pairs):
+        for j in range(3):
+            w_local(t, j).start()
+    local(w_out, WO, 2).start()
 
     barrier = pltpu.get_barrier_semaphore()
     peers = [
@@ -161,46 +172,47 @@
 
     def chunk(e, core):
         is_last = e >= first_last
-        idx = jnp.where(is_last, opp, 2 * lax.div(e, 4) + core)
-        j = jnp.where(is_last, 2 * core + e - first_last, lax.rem(e, 4))
-        return idx, j
+        k = lax.rem(e, 4)
+        direction = lax.rem(k, 2)
+        part = jnp.where(is_last, direction, lax.div(k, 2))
+        idx = jnp.where(is_last, opp, 2 * lax.div(e, 4) + direction)
+        return idx, 2 * core + part, direction, part
 
     def row_of(j, parity):
         return pl.multiple_of(parity * half + j * ch, ch)
 
-    def z_copy(src, idx, j, e):
+    def z_copy(src, idx, j, direction, e):
         return remote(
             src,
             X.at[idx, pl.ds(row_of(j, par), ch)],
             zs.at[e],
             zr.at[e],
-            {"seq": z_next},
+            {"seq": lax.rem(z + 1 - 2 * direction + n_seq, n_seq)},
         )
 
     def x_copy(e, parity):
-        idx, j = chunk(e, c)
-        back = jnp.where(e >= first_last, e - first_last, lax.div(j, 2))
+        idx, j, _, part = chunk(e, c)
         ref = X.at[idx, pl.ds(row_of(j, parity), ch)]
-        to = lax.rem(x + 1 - 2 * back + n_ten, n_ten)
+        to = lax.rem(x + 1 - 2 * part + n_ten, n_ten)
         return remote(ref, ref, xs.at[e], xr.at[e], {"tensor": to})
 
     def d_copy(e, core, parity, ssem, rsem):
-        idx, j = chunk(e, core)
+        idx, j, _, _ = chunk(e, core)
         ref = X.at[idx, pl.ds(row_of(j, parity), ch)]
         return remote(ref, ref, ssem.at[e], rsem.at[e], {"cfg": 1 - c})
 
     def z_event(e):
-        idx, j = chunk(e, c)
+        idx, j, direction, part = chunk(e, c)
         here = X.at[idx, pl.ds(row_of(j, par), ch)]
-        z_copy(here, idx, j, e).wait_recv()
-        going = (e < first_last - 4) | ((e < first_last) & (lax.div(j, 2) == c))
+        z_copy(here, idx, j, direction, e).wait_recv()
+        going = (e < first_last - 4) | ((e < first_last) & (part == direction))
 
         @pl.when(going)
         def _():
             far = e >= first_last - 4
-            ne = jnp.where(far, first_last + j - 2 * c, e + 4)
+            ne = jnp.where(far, first_last + direction, e + 4)
             nidx = jnp.where(far, opp, idx + 2)
-            z_copy(here, nidx, j, ne).start()
+            z_copy(here, nidx, j, direction, ne).start()
 
         x_copy(e, par).start()
         d_copy(e, c, par, dzs, dzr).start()
@@ -208,15 +220,17 @@
     def x_event(e):
         x_copy(e, 1 - par).wait_recv()
         d_copy(e, c, 1 - par, dxs, dxr).start()
+
+    lag = 4
 
     def event(e):
         @pl.when(e < n_ev)
         def _():
             z_event(e)
 
-        @pl.when((e >= 2) & (e < n_ev + 2))
+        @pl.when((e >= lag) & (e < n_ev + lag))
         def _():
-            x_event(e - 2)
+            x_event(e - lag)
 
     def t_copies(src, idx, direction):
         to = {"seq": z_down if direction else z_up}
@@ -240,21 +254,31 @@
                     for copy in t_copies(idx, nxt, direction):
                         copy.start()
 
-    for j in range(4):
-        z_copy(latent.at[pl.ds(row_of(j, par), ch)], c, j, j).start()
-    w_copies = [
-        remote(w_qkv.at[j], W.at[j, mine_k], wsend.at[j], wrecv.at[j], {"cfg": 1 - c})
-        for j in range(3)
-    ]
-    w_copies[2].start()
-    local(text_kv.at[0], T.at[own], 4).wait()
+    for k in range(4):
+        j = 2 * c + k // 2
+        z_copy(latent.at[pl.ds(row_of(j, par), ch)], k % 2, j, k % 2, k).start()
+    def w_remote(t, j, k_rows):
+        at = 3 * t + j
+        return remote(
+            w_from(t, j),
+            W.at[t, k_rows, pl.ds(j * pair, pair)],
+            wsend.at[at],
+            wrecv.at[at],
+            {"cfg": 1 - c},
+        )
+
+    for j in range(3):
+        w_remote(0, j, mine_k).start()
+    local(text_kv.at[0], T.at[own], 1).wait()
     t_copies(own, 0, 0)[0].start()
     t_copies(own, 1, 1)[0].start()
-    w_copies[1].start()
-    w_copies[0].start()
-
-    local(latent, X.at[own], 3).wait()
-    xf = X[own].astype(F32)
+    for t in range(1, pairs):
+        for j in range(3):
+            w_remote(t, j, mine_k).start()
+
+    local(latent, XO.at[pl.ds(0, rows)], 0).wait()
+    XO[rows : rows + 16] = jnp.ones((16, d), BF16)
+    xf = XO[0:rows].astype(F32)
     mean = jnp.mean(xf, axis=-1, keepdims=True)
     center = xf - mean
     rstd = lax.rsqrt(jnp.mean(center * center, axis=-1, keepdims=True) + 1e-06)
@@ -271,7 +295,7 @@
 
     kt = 256
 
-    def fold(j, part):
+    def fold(t, part):
         def body(i, carry):
             base = pl.multiple_of(part * kdev + i * kt, kt)
             shift_row = modulation[0, pl.ds(c, 1), pl.ds(base, kt)]
@@ -279,31 +303,22 @@
             srow = lax.broadcasted_iota(jnp.int32, (8, kt), 0)
             both = jnp.where(srow == 0, 1.0 + scale_row, jnp.where(srow == 1, shift_row, 0.0))
             cols = jnp.transpose(both)
-            raw = W[j, pl.ds(base, kt), :].astype(F32)
-            new = (raw * cols[:, 0:1]).astype(BF16)
-            W[j, pl.ds(base, kt), :] = new
-            cs[j] += jnp.sum(new.astype(F32).reshape(kt // 8, 8, width), axis=0)
-            bw[j] += jnp.sum((raw * cols[:, 1:2]).reshape(kt // 8, 8, width), axis=0)
+            raw = W[t, pl.ds(base, kt), :].astype(F32)
+            W[t, pl.ds(base, kt), :] = (raw * cols[:, 0:1]).astype(BF16)
+            bw[t] += jnp.sum((raw * cols[:, 1:2]).reshape(kt // 8, 8, 3 * pair), axis=0)
             return carry
 
         lax.fori_loop(0, kdev // kt, body, 0)
 
-    def finish(j):
-        cs[j] = jnp.broadcast_to(jnp.sum(cs[j], axis=0, keepdims=True), (8, width))
-        bw[j] = jnp.broadcast_to(jnp.sum(bw[j], axis=0, keepdims=True), (8, width))
-
-    cs[...] = jnp.zeros_like(cs)
     bw[...] = jnp.zeros_like(bw)
     acc[...] = jnp.zeros_like(acc)
     lsum[...] = jnp.zeros_like(lsum)
-    for j in (2, 1, 0):
-        local(w_qkv.at[j], W.at[j, mine_k], j).wait()
-        fold(j, c)
-
-    def w_arrive(j):
-        remote(w_qkv.at[j], W.at[j, other_k], wsend.at[j], wrecv.at[j], {"cfg": 1 - c}).wait_recv()
-        fold(j, 1 - c)
-        finish(j)
+
+    def w_arrive(t):
+        for j in range(3):
+            w_remote(t, j, other_k).wait_recv()
+        fold(t, 1 - c)
+        bw[t] = jnp.broadcast_to(jnp.sum(bw[t], axis=0, keepdims=True), (8, 3 * pair))
 
     def tables(idx, at):
         a = A[idx]
@@ -323,70 +338,79 @@
             hot, table[TABLE_ROWS : 2 * TABLE_ROWS]
         )
 
-    def affine(block, j, lanes, m):
-        return block * ST[0, 0:m] - ST[1, 0:m] * cs[j, 0:1, lanes] + bw[j, 0:1, lanes]
-
-    def head_rows(block, j, lanes, m, gain):
-        v = affine(block, j, lanes, m)
+    q_gain = gains[0:1, :]
+    k_gain = gains[1:2, :]
+
+    def affine(block, t, lanes, m):
+        return block * ST[0, 0:m] - ST[1, 0:m] * cs[t, 0:1, lanes] + bw[t, 0:1, lanes]
+
+    def head_rows(block, t, lanes, m, gain):
+        v = affine(block, t, lanes, m)
         r = lax.rsqrt(jnp.mean(v * v, axis=-1, keepdims=True) + 1e-06)
         v = v * gain
         v = v * CT[0:m, 0:HEAD_DIM] + partner_lanes(v) * CT[0:m, HEAD_DIM : 2 * HEAD_DIM]
-        return (v * r).astype(BF16)
-
-    q_gain = gains[0:1, :]
-    k_gain = gains[1:2, :]
+        return v * r
 
     def attend(h, keys, values, m, mask=None):
-        s = contract_last(Q[h], keys)
-        p = jnp.exp2(s * scale)
+        p = jnp.exp2(jnp.dot(keys, Q[h], preferred_element_type=F32) * scale)
         if mask is not None:
             p = jnp.where(mask, p, 0.0)
-        part = p[:, 0:HEAD_DIM]
-        for k in range(1, m // HEAD_DIM):
-            part = part + p[:, k * HEAD_DIM : (k + 1) * HEAD_DIM]
-        lsum[h] += part
-        acc[h] += jnp.dot(p.astype(BF16), values, preferred_element_type=F32)
-
-    pair = 2 * HEAD_DIM
+        lsum[h] += jnp.sum(p.reshape(m // 8, 8, rows), axis=0)
+        acc[h] += contract_first(values, p.astype(BF16))
+
+    def lanes_of(j, hh):
+        return slice(j * pair + hh * HEAD_DIM, j * pair + (hh + 1) * HEAD_DIM)
+
+    def attend_pair(kv, t, m, skip):
+        for hh in range(2):
+            kl, vl = lanes_of(1, hh), lanes_of(2, hh)
+            k_in = slice(kl.start - skip, kl.stop - skip)
+            v_in = slice(vl.start - skip, vl.stop - skip)
+            keys = head_rows(kv[0:m, k_in], t, kl, m, k_gain).astype(BF16)
+            values = affine(kv[0:m, v_in], t, vl, m).astype(BF16)
+            attend(2 * t + hh, keys, values, m)
 
     def key_values(load, t, m):
-        wide = slice(t * pair, (t + 1) * pair)
-        k2 = jnp.dot(load(), W[1, :, wide], preferred_element_type=F32)
-        v2 = jnp.dot(load(), W[2, :, wide], preferred_element_type=F32)
+        kv = jnp.dot(load(), W[t, :, pair : 3 * pair], preferred_element_type=F32)
+        attend_pair(kv, t, m, pair)
+
+    def own_dot(t):
+        OW[t % 2] = jnp.dot(XO[...], W[t], preferred_element_type=F32)
+
+    def own_pair(t):
+        qkv = OW.at[t % 2]
+        cs[t] = qkv[rows : rows + 8]
         for hh in range(2):
-            h = 2 * t + hh
-            lanes = slice(h * HEAD_DIM, (h + 1) * HEAD_DIM)
-            sub_l = slice(hh * HEAD_DIM, (hh + 1) * HEAD_DIM)
-            keys = head_rows(k2[:, sub_l], 1, lanes, m, k_gain)
-            values = affine(v2[:, sub_l], 2, lanes, m).astype(BF16)
-            attend(h, keys, values, m)
-
-    event(0)
-    w_arrive(2)
+            ql = lanes_of(0, hh)
+            q = head_rows(qkv[0:rows, ql], t, ql, rows, q_gain)
+            Q[2 * t + hh] = jnp.transpose(q).astype(BF16)
+        attend_pair(qkv, t, rows, 0)
+
     tables(own, 0)
+    for t in range(pairs):
+        for j in range(3):
+            w_local(t, j).wait()
+        fold(t, c)
+        if t == 0:
+            event(0)
     event(1)
     text_event(1)
-    w_arrive(1)
-    event(2)
-    w_arrive(0)
-    event(3)
-    for t in range(heads // 2):
-        wide = slice(t * pair, (t + 1) * pair)
-        q2 = jnp.dot(X[own], W[0, :, wide], preferred_element_type=F32)
-        for hh in range(2):
-            h = 2 * t + hh
-            lanes = slice(h * HEAD_DIM, (h + 1) * HEAD_DIM)
-            Q[h] = head_rows(
-                q2[:, hh * HEAD_DIM : (hh + 1) * HEAD_DIM], 0, lanes, rows, q_gain
-            )
-    event(4)
-    for t in range(heads // 2):
-        key_values(lambda: X[own], t, rows)
-    event(5)
+    for t in range(pairs):
+        w_arrive(t)
+        event(2 * t + 2)
+        own_dot(t)
+        if t > 0:
+            own_pair(t - 1)
+        event(2 * t + 3)
+    own_pair(pairs - 1)
 
     def wait_partner(e):
         d_copy(e, 1 - c, par, dzs, dzr).wait_recv()
         d_copy(e, 1 - c, 1 - par, dxs, dxr).wait_recv()
+
+    def pair_dot(base, t):
+        both = X[pl.ds(base, 2)].reshape(2 * rows, d)
+        KV[t % 2] = jnp.dot(both, W[t, :, pair : 3 * pair], preferred_element_type=F32)
 
     def step(s, carry):
         def waits(k, carry):
@@ -395,27 +419,31 @@
 
         lax.fori_loop(0, 4, waits, 0)
         base = pl.multiple_of(2 * (s - 1), 2)
+        event(4 * s + 4)
         tables(base, 0)
         tables(base + 1, rows)
-        for t in range(heads // 2):
-            key_values(lambda: X[pl.ds(base, 2)].reshape(2 * rows, d), t, 2 * rows)
-            event(4 * s + 2 + t)
+        pair_dot(base, 0)
+        event(4 * s + 5)
+        for t in range(1, pairs):
+            pair_dot(base, t)
+            attend_pair(KV.at[(t - 1) % 2], t - 1, 2 * rows, pair)
+            event(4 * s + 5 + t)
+        attend_pair(KV.at[(pairs - 1) % 2], pairs - 1, 2 * rows, pair)
         text_event(s + 1)
-        event(4 * s + 5)
         return carry
 
     lax.fori_loop(1, last_step, step, 0)
 
-    key_lane = lax.broadcasted_iota(jnp.int32, (1, n_seq * T.shape[2]), 1)
     trows = T.shape[2]
-    slot = lax.div(key_lane, trows)
+    m_text = n_seq * trows
+    key_row = lax.broadcasted_iota(jnp.int32, (m_text, rows), 0)
+    slot = lax.div(key_row, trows)
     away = lax.div(slot, 2) + 1
     sign = 1 - 2 * lax.rem(slot, 2)
     plane = lax.rem(z - sign * away + 2 * n_seq, n_seq)
     plane = jnp.where(slot == own, z, plane)
     plane = jnp.where(slot == opp, lax.rem(z + last_step, n_seq), plane)
-    used = plane * trows + lax.rem(key_lane, trows) < text_len[0]
-    m_text = n_seq * trows
+    used = plane * trows + lax.rem(key_row, trows) < text_len[0]
     for h in range(heads):
         lanes = slice(h * HEAD_DIM, (h + 1) * HEAD_DIM)
         tk = T[:, 0, :, lanes].reshape(m_text, HEAD_DIM).astype(F32)
@@ -426,15 +454,16 @@
     wait_partner(first_last)
     wait_partner(first_last + 1)
     tables(opp, 0)
-    for t in range(heads // 2):
+    for t in range(pairs):
         key_values(lambda: X[opp], t, rows)
 
     for h in range(heads):
-        total = jnp.sum(lsum[h], axis=-1, keepdims=True)
-        att[0, :, h * HEAD_DIM : (h + 1) * HEAD_DIM] = (acc[h] / total).astype(BF16)
+        total = jnp.sum(lsum[h], axis=0, keepdims=True)
+        mixed = jnp.transpose(acc[h] / total)
+        att[0, :, h * HEAD_DIM : (h + 1) * HEAD_DIM] = mixed.astype(BF16)
     swap = remote(att.at[0], att.at[1], asend.at[0], arecv.at[0], {"cfg": 1 - c})
     swap.start()
-    local(w_out, WO, 5).wait()
+    local(w_out, WO, 2).wait()
     ocols = w_out.shape[1]
     mine_o = pl.multiple_of(c * ocols, ocols)
     nt = ocols // 3
@@ -481,15 +510,16 @@
     for t in range(3):
         for k in (1, 2, 3):
             g_copy(k, t).wait_send()
-    for j in range(3):
-        w_copies[j].wait_send()
+    for t in range(pairs):
+        for j in range(3):
+            w_remote(t, j, mine_k).wait_send()
 
     def sent(e, carry):
         x_copy(e, par).wait_send()
         d_copy(e, c, par, dzs, dzr).wait_send()
         d_copy(e, c, 1 - par, dxs, dxr).wait_send()
-        idx, j = chunk(e, c)
-        z_copy(X.at[idx, pl.ds(row_of(j, par), ch)], idx, j, e).wait_send()
+        idx, j, direction, _ = chunk(e, c)
+        z_copy(X.at[idx, pl.ds(row_of(j, par), ch)], idx, j, direction, e).wait_send()
         return carry
 
     lax.fori_loop(0, n_ev, sent, 0)
@@ -531,24 +561,26 @@
             ],
             out_specs=spec(vmem),
             scratch_shapes=[
-                vmem((n_seq, rows, d), BF16),
-                vmem((3, d, width), BF16),
+                vmem((n_seq - 1, rows, d), BF16),
+                vmem((rows + 16, d), BF16),
+                vmem((heads // 2, d, 6 * HEAD_DIM), BF16),
                 vmem((width, ocols), BF16),
                 vmem((n_seq, 2, text_kv.shape[2], width), BF16),
                 vmem((n_seq, 8, rows), F32),
-                vmem((heads, rows, HEAD_DIM), BF16),
+                vmem((heads, HEAD_DIM, rows), BF16),
                 vmem((2 * rows, 2 * HEAD_DIM), F32),
                 vmem((2, 2 * rows, HEAD_DIM), F32),
-                vmem((3, 8, width), F32),
-                vmem((3, 8, width), F32),
-                vmem((heads, rows, HEAD_DIM), F32),
-                vmem((heads, rows, HEAD_DIM), F32),
-                vmem((8, 128), F32),
+                vmem((heads // 2, 8, 6 * HEAD_DIM), F32),
+                vmem((heads // 2, 8, 6 * HEAD_DIM), F32),
+                vmem((heads, HEAD_DIM, rows), F32),
+                vmem((heads, 8, rows), F32),
+                vmem((2, 2 * rows, 4 * HEAD_DIM), F32),
+                vmem((2, rows + 16, 6 * HEAD_DIM), F32),
                 vmem((2, rows, width), BF16),
                 vmem((rows, ocols), F32),
                 vmem((rows, ocols), BF16),
                 vmem((n_ten - 1, rows // n_ten, ocols), BF16),
-                dma((6,)),
+                dma((12,)),
                 dma((n_ev,)),
                 dma((n_ev,)),
                 dma((n_ev,)),
@@ -561,8 +593,8 @@
                 dma((n_seq,)),
                 dma((n_seq,)),
                 dma((n_seq,)),
-                dma((3,)),
-                dma((3,)),
+                dma((9,)),
+                dma((9,)),
                 dma((1,)),
                 dma((1,)),
                 dma((9,)),

time: 190 us -> 149 us (0.78)
  Pallas kernels: 187 us -> 146 us
    pallas_call x1, Pallas kernels: 187 us -> 146 us  [local(): pl.pallas_call(functools.partial(kernel, (n_seq, n_ten)), out_shape=jax.S...]
where the time goes in v2:
time: 149 us
  Pallas kernels  146 us (98%)
  local copies, waits for them, and re-layouts  1.62 us (1%)
    pallas_call x1, Pallas kernels, local(): pl.pallas_call(functools.partial(kernel, (n_seq, n_ten)), out_shape=jax.S...  146 us

profile of v2, /device:TPU:33, one launch (start us, length us, event | category | flops | bytes accessed | tf_op | source)
XLA Modules:
  0.0 149.3 jit_solution(4616756619353521107)
XLA Ops:
  1.3 146.3 %shard_map.100 = bf16[64,1536]{1,0:T(8,128)(2,1)} custom-call(bf16[256,3072]{1,0:T(8,128)(2,1)} %latent.1, s32[3,256]{1,0:T(4,128)} %positions.1, bf16[1,2,16,768]{3,2,1,0:T(8,128)(2,1)} %text_kv.1, s32[1]{0:T(128)S(6)} %copy.12.text_len, f32[3,2,3072]{2,1,0:T(2,128)} %modulation.1, bf16[3,1536,768]{2,1,0:T(8,128)(2,1)} %w_qkv.1, f32[2,128]{1,0:T(2,128)} %gains.1, ...), custom_call_target="tpu_custom_call" | custom-call | tf_op jit(solution)/shard_map/pallas_call | solution.py:547
  147.6 1.6 %copy.14 = bf16[64,1536]{1,0:T(8,128)(2,1)} copy(bf16[64,1536]{1,0:T(8,128)(2,1)} %shard_map.100) | data formatting | bytes 393216

commit v3 on v2

--- a/solution.py
+++ b/solution.py
@@ -158,6 +158,7 @@
         for j in range(3):
             w_local(t, j).start()
     local(w_out, WO, 2).start()
+    local(latent, X.at[own], 12).start()
 
     barrier = pltpu.get_barrier_semaphore()
     peers = [
@@ -320,13 +321,13 @@
         fold(t, 1 - c)
         bw[t] = jnp.broadcast_to(jnp.sum(bw[t], axis=0, keepdims=True), (8, 3 * pair))
 
-    def tables(idx, at):
+    def tables(idx, at, q):
         a = A[idx]
         cols = jnp.transpose(a)
         at_rows = pl.ds(at, rows)
         rs = cols[:, 4:5]
-        ST[0, at_rows] = jnp.broadcast_to(rs, (rows, HEAD_DIM))
-        ST[1, at_rows] = jnp.broadcast_to(cols[:, 3:4] * rs, (rows, HEAD_DIM))
+        ST[q, 0, at_rows] = jnp.broadcast_to(rs, (rows, HEAD_DIM))
+        ST[q, 1, at_rows] = jnp.broadcast_to(cols[:, 3:4] * rs, (rows, HEAD_DIM))
         index = lax.broadcasted_iota(jnp.int32, (TABLE_ROWS, rows), 0).astype(F32)
         hot = (
             (index == a[0:1] + float(STARTS[0]))
@@ -334,21 +335,21 @@
             | (index == a[2:3] + float(STARTS[2]))
         )
         hot = jnp.where(hot, 1.0, 0.0).astype(BF16)
-        CT[at_rows] = contract_first(hot, table[0:TABLE_ROWS]) + contract_first(
+        CT[q, at_rows] = contract_first(hot, table[0:TABLE_ROWS]) + contract_first(
             hot, table[TABLE_ROWS : 2 * TABLE_ROWS]
         )
 
     q_gain = gains[0:1, :]
     k_gain = gains[1:2, :]
 
-    def affine(block, t, lanes, m):
-        return block * ST[0, 0:m] - ST[1, 0:m] * cs[t, 0:1, lanes] + bw[t, 0:1, lanes]
-
-    def head_rows(block, t, lanes, m, gain):
-        v = affine(block, t, lanes, m)
+    def affine(block, t, lanes, m, q):
+        return block * ST[q, 0, 0:m] - ST[q, 1, 0:m] * cs[t, 0:1, lanes] + bw[t, 0:1, lanes]
+
+    def head_rows(block, t, lanes, m, gain, q):
+        v = affine(block, t, lanes, m, q)
         r = lax.rsqrt(jnp.mean(v * v, axis=-1, keepdims=True) + 1e-06)
         v = v * gain
-        v = v * CT[0:m, 0:HEAD_DIM] + partner_lanes(v) * CT[0:m, HEAD_DIM : 2 * HEAD_DIM]
+        v = v * CT[q, 0:m, 0:HEAD_DIM] + partner_lanes(v) * CT[q, 0:m, HEAD_DIM : 2 * HEAD_DIM]
         return v * r
 
     def attend(h, keys, values, m, mask=None):
@@ -361,18 +362,14 @@
     def lanes_of(j, hh):
         return slice(j * pair + hh * HEAD_DIM, j * pair + (hh + 1) * HEAD_DIM)
 
-    def attend_pair(kv, t, m, skip):
+    def attend_pair(kv, t, m, skip, q):
         for hh in range(2):
             kl, vl = lanes_of(1, hh), lanes_of(2, hh)
             k_in = slice(kl.start - skip, kl.stop - skip)
             v_in = slice(vl.start - skip, vl.stop - skip)
-            keys = head_rows(kv[0:m, k_in], t, kl, m, k_gain).astype(BF16)
-            values = affine(kv[0:m, v_in], t, vl, m).astype(BF16)
+            keys = head_rows(kv[0:m, k_in], t, kl, m, k_gain, q).astype(BF16)
+            values = affine(kv[0:m, v_in], t, vl, m, q).astype(BF16)
             attend(2 * t + hh, keys, values, m)
-
-    def key_values(load, t, m):
-        kv = jnp.dot(load(), W[t, :, pair : 3 * pair], preferred_element_type=F32)
-        attend_pair(kv, t, m, pair)
 
     def own_dot(t):
         OW[t % 2] = jnp.dot(XO[...], W[t], preferred_element_type=F32)
@@ -382,11 +379,11 @@
         cs[t] = qkv[rows : rows + 8]
         for hh in range(2):
             ql = lanes_of(0, hh)
-            q = head_rows(qkv[0:rows, ql], t, ql, rows, q_gain)
-            Q[2 * t + hh] = jnp.transpose(q).astype(BF16)
-        attend_pair(qkv, t, rows, 0)
-
-    tables(own, 0)
+            query = head_rows(qkv[0:rows, ql], t, ql, rows, q_gain, 0)
+            Q[2 * t + hh] = jnp.transpose(query).astype(BF16)
+        attend_pair(qkv, t, rows, 0, 0)
+
+    tables(own, 0, 0)
     for t in range(pairs):
         for j in range(3):
             w_local(t, j).wait()
@@ -402,60 +399,82 @@
         if t > 0:
             own_pair(t - 1)
         event(2 * t + 3)
-    own_pair(pairs - 1)
-
     def wait_partner(e):
         d_copy(e, 1 - c, par, dzs, dzr).wait_recv()
         d_copy(e, 1 - c, 1 - par, dxs, dxr).wait_recv()
 
     def pair_dot(base, t):
         both = X[pl.ds(base, 2)].reshape(2 * rows, d)
-        KV[t % 2] = jnp.dot(both, W[t, :, pair : 3 * pair], preferred_element_type=F32)
+        KV[t] = jnp.dot(both, W[t, :, pair : 3 * pair], preferred_element_type=F32)
+
+    def begin(s):
+        def waits(k, carry):
+            e = 4 * (s - 1) + k
+
+            @pl.when(e < n_ev)
+            def _():
+                wait_partner(e)
+
+            return carry
+
+        lax.fori_loop(0, 4, waits, 0)
+
+    def first_dot(s, q):
+        base = pl.multiple_of(2 * (s - 1), 2)
+        tables(base, 0, q)
+        tables(base + 1, rows, q)
+        pair_dot(base, 0)
+
+    last = pairs - 1
+    local(latent, X.at[own], 12).wait()
+    begin(1)
+    first_dot(1, 1)
+    own_pair(last)
+
+    def prompt_rows():
+        trows = T.shape[2]
+        m_text = n_seq * trows
+        key_row = lax.broadcasted_iota(jnp.int32, (m_text, rows), 0)
+        slot = lax.div(key_row, trows)
+        away = lax.div(slot, 2) + 1
+        sign = 1 - 2 * lax.rem(slot, 2)
+        plane = lax.rem(z - sign * away + 2 * n_seq, n_seq)
+        plane = jnp.where(slot == own, z, plane)
+        plane = jnp.where(slot == opp, lax.rem(z + last_step, n_seq), plane)
+        used = plane * trows + lax.rem(key_row, trows) < text_len[0]
+        for h in range(heads):
+            lanes = slice(h * HEAD_DIM, (h + 1) * HEAD_DIM)
+            tk = T[:, 0, :, lanes].reshape(m_text, HEAD_DIM).astype(F32)
+            r = lax.rsqrt(jnp.mean(tk * tk, axis=-1, keepdims=True) + 1e-06)
+            keys = (tk * r * k_gain).astype(BF16)
+            attend(h, keys, T[:, 1, :, lanes].reshape(m_text, HEAD_DIM), m_text, used)
 
     def step(s, carry):
-        def waits(k, carry):
-            wait_partner(4 * (s - 1) + k)
-            return carry
-
-        lax.fori_loop(0, 4, waits, 0)
         base = pl.multiple_of(2 * (s - 1), 2)
-        event(4 * s + 4)
-        tables(base, 0)
-        tables(base + 1, rows)
-        pair_dot(base, 0)
-        event(4 * s + 5)
+        q = lax.rem(s, 2)
         for t in range(1, pairs):
+            event(4 * s + 3 + t)
             pair_dot(base, t)
-            attend_pair(KV.at[(t - 1) % 2], t - 1, 2 * rows, pair)
-            event(4 * s + 5 + t)
-        attend_pair(KV.at[(pairs - 1) % 2], pairs - 1, 2 * rows, pair)
+            attend_pair(KV.at[t - 1], t - 1, 2 * rows, pair, q)
+        event(4 * s + 6)
         text_event(s + 1)
+        event(4 * s + 7)
+
+        @pl.when(s == last_step - 1)
+        def _():
+            prompt_rows()
+
+        begin(s + 1)
+        first_dot(s + 1, 1 - q)
+        attend_pair(KV.at[last], last, 2 * rows, pair, q)
         return carry
 
     lax.fori_loop(1, last_step, step, 0)
 
-    trows = T.shape[2]
-    m_text = n_seq * trows
-    key_row = lax.broadcasted_iota(jnp.int32, (m_text, rows), 0)
-    slot = lax.div(key_row, trows)
-    away = lax.div(slot, 2) + 1
-    sign = 1 - 2 * lax.rem(slot, 2)
-    plane = lax.rem(z - sign * away + 2 * n_seq, n_seq)
-    plane = jnp.where(slot == own, z, plane)
-    plane = jnp.where(slot == opp, lax.rem(z + last_step, n_seq), plane)
-    used = plane * trows + lax.rem(key_row, trows) < text_len[0]
-    for h in range(heads):
-        lanes = slice(h * HEAD_DIM, (h + 1) * HEAD_DIM)
-        tk = T[:, 0, :, lanes].reshape(m_text, HEAD_DIM).astype(F32)
-        r = lax.rsqrt(jnp.mean(tk * tk, axis=-1, keepdims=True) + 1e-06)
-        keys = (tk * r * k_gain).astype(BF16)
-        attend(h, keys, T[:, 1, :, lanes].reshape(m_text, HEAD_DIM), m_text, used)
-
-    wait_partner(first_last)
-    wait_partner(first_last + 1)
-    tables(opp, 0)
     for t in range(pairs):
-        key_values(lambda: X[opp], t, rows)
+        if t > 0:
+            KV[t, 0:rows] = jnp.dot(X[opp], W[t, :, pair : 3 * pair], preferred_element_type=F32)
+        attend_pair(KV.at[t], t, rows, pair, last_step % 2)
 
     for h in range(heads):
         total = jnp.sum(lsum[h], axis=0, keepdims=True)
@@ -561,26 +580,26 @@
             ],
             out_specs=spec(vmem),
             scratch_shapes=[
-                vmem((n_seq - 1, rows, d), BF16),
+                vmem((n_seq, rows, d), BF16),
                 vmem((rows + 16, d), BF16),
                 vmem((heads // 2, d, 6 * HEAD_DIM), BF16),
                 vmem((width, ocols), BF16),
                 vmem((n_seq, 2, text_kv.shape[2], width), BF16),
                 vmem((n_seq, 8, rows), F32),
                 vmem((heads, HEAD_DIM, rows), BF16),
-                vmem((2 * rows, 2 * HEAD_DIM), F32),
-                vmem((2, 2 * rows, HEAD_DIM), F32),
+                vmem((2, 2 * rows, 2 * HEAD_DIM), F32),
+                vmem((2, 2, 2 * rows, HEAD_DIM), F32),
                 vmem((heads // 2, 8, 6 * HEAD_DIM), F32),
                 vmem((heads // 2, 8, 6 * HEAD_DIM), F32),
                 vmem((heads, HEAD_DIM, rows), F32),
                 vmem((heads, 8, rows), F32),
-                vmem((2, 2 * rows, 4 * HEAD_DIM), F32),
+                vmem((heads // 2, 2 * rows, 4 * HEAD_DIM), F32),
                 vmem((2, rows + 16, 6 * HEAD_DIM), F32),
                 vmem((2, rows, width), BF16),
                 vmem((rows, ocols), F32),
                 vmem((rows, ocols), BF16),
                 vmem((n_ten - 1, rows // n_ten, ocols), BF16),
-                dma((12,)),
+                dma((13,)),
                 dma((n_ev,)),
                 dma((n_ev,)),
                 dma((n_ev,)),

time: 149 us -> 150 us (level)
  no operation moved by 1% of the time
where the time goes in v3:
time: 150 us
  Pallas kernels  147 us (98%)
  local copies, waits for them, and re-layouts  1.62 us (1%)
    pallas_call x1, Pallas kernels, local(): pl.pallas_call(functools.partial(kernel, (n_seq, n_ten)), out_shape=jax.S...  147 us

profile of v3, /device:TPU:33, one launch (start us, length us, event | category | flops | bytes accessed | tf_op | source)
XLA Modules:
  0.0 149.9 jit_solution(13569656762271427518)
XLA Ops:
  1.3 147.0 %shard_map.100 = bf16[64,1536]{1,0:T(8,128)(2,1)} custom-call(bf16[256,3072]{1,0:T(8,128)(2,1)} %latent.1, s32[3,256]{1,0:T(4,128)} %positions.1, bf16[1,2,16,768]{3,2,1,0:T(8,128)(2,1)} %text_kv.1, s32[1]{0:T(128)S(6)} %copy.12.text_len, f32[3,2,3072]{2,1,0:T(2,128)} %modulation.1, bf16[3,1536,768]{2,1,0:T(8,128)(2,1)} %w_qkv.1, f32[2,128]{1,0:T(2,128)} %gains.1, ...), custom_call_target="tpu_custom_call" | custom-call | tf_op jit(solution)/shard_map/pallas_call | solution.py:566
  148.3 1.6 %copy.14 = bf16[64,1536]{1,0:T(8,128)(2,1)} copy(bf16[64,1536]{1,0:T(8,128)(2,1)} %shard_map.100) | data formatting | bytes 393216
